TPU v7x, 32 devices: a whole 2x2x4 slice. The times are simulated.
32 devices in a mesh: tm: 8 (over z, y), mp: 4 (over x, core).
Axes of the slice: x: 2, y: 2, z: 4, core: 2. Of those that a mesh axis runs over, the one named last changes fastest.
Arguments:
- latents: float32 [4, 8, 4, 4096], P(None, 'tm'), may hold values from -6 to 6
- noise: float32 [4, 8, 4, 4096], P(None, 'tm'), may hold values from -6 to 6
- start_step: int32 [4], replicated, may hold values from 8 to 999
- slide: int32 [4], replicated, may hold values from 1 to 8, as said below
- w_in: float32 [4, 320], replicated, may hold values from -3 to 3
- w_gate: bfloat16 [320, 1280], P(None, 'mp'), may hold values from -0.3125 to 0.3125
- w_value: bfloat16 [320, 1280], P(None, 'mp'), may hold values from -0.3125 to 0.3125
- w_down: bfloat16 [1280, 320], P('mp'), may hold values from -0.15625 to 0.15625
- w_out: float32 [320, 4], replicated, may hold values from -0.3125 to 0.3125
Outputs:
- next_window: float32 [4, 8, 4, 4096], P(None, 'tm')
- eps: float32 [4, 8, 4, 4096], P(None, 'tm', None, 'mp')
Inputs may be any that keep to these rules, and one draw needn't show every extreme that they name: `slide`: some prompt slides by exactly 8, and another by exactly 1.
All inputs are finite; a program needn't handle non-finite values.
Results may differ from a plain program's by a relative error of at most 0.0023.
Values sent between devices are 32-bit elements; how exact they have to be, the bound alone decides.
No kernel may reach another device: no remote copies, remote signals or barrier semaphores. Data moves between devices by JAX's collectives and lax.ppermute only.
A program may use at most 64 MiB of HBM per device.

v0:
```python
import math
import jax
import jax.numpy as jnp
from jax import lax
from jax.sharding import PartitionSpec as P

TSTEPS = 1000


def prefix(x, axis, combine, identity):
    peers, mine = (lax.axis_size(axis), lax.axis_index(axis))
    everything = lax.all_gather(x, axis)
    start = jnp.broadcast_to(jnp.asarray(identity, x.dtype), x.shape)

    def lap(k, before):
        reached = k < mine
        new = combine(before, everything[k])
        return jnp.where(reached, new, before)

    return lax.fori_loop(0, peers, lap, start)


def from_root(block, axis, holder):
    block = jnp.where(lax.axis_index(axis) == holder, block, jnp.zeros_like(block))
    return lax.psum(block, axis)


def from_behind(block, axis, distance):
    devices = range(lax.axis_size(axis))
    route = [(i - distance, i) for i in devices if i - distance in devices]
    return lax.ppermute(block, axis, route)


def plan(count):
    steps_f = jnp.arange(count, dtype=jnp.float32)
    beta = 0.0001 + (0.02 - 0.0001) * steps_f / (count - 1)
    abar = jnp.cumprod(1.0 - beta)
    return (beta, abar)


def lookup(table, times):
    grid = jnp.arange(table.shape[0], dtype=jnp.int32)
    return jnp.sum(jnp.where(times[..., None] == grid, table, 0.0), axis=-1)


def embed(times, channels):
    half = channels // 2
    freq = jnp.exp(-math.log(10000.0) * jnp.arange(half, dtype=jnp.float32) / half)
    angle = times[..., None] * freq
    return jnp.concatenate([jnp.cos(angle), jnp.sin(angle)], axis=-1)


def add_terms(earlier, later):
    return earlier + later


def shards(latents, noise, start_step, slide, w_in, w_gate, w_value, w_down, w_out):
    prompts, t_dev, lat, pos = latents.shape
    channels = w_in.shape[1]
    n_tm = lax.axis_size("tm")
    window = n_tm * t_dev
    share_width = pos // lax.axis_size("mp")
    share_offset = lax.axis_index("mp") * share_width
    slots = lax.axis_index("tm") * t_dev + jnp.arange(t_dev, dtype=jnp.int32)
    times = start_step[:, None] - slots[None, :]
    beta, abar = plan(TSTEPS)
    beta_t = lookup(beta, times)[:, :, None, None]
    abar_t = lookup(abar, times)[:, :, None, None]
    vectors = embed(times.astype(jnp.float32), channels).reshape(prompts * t_dev, channels)
    folded = jnp.dot(w_down.astype(jnp.float32), w_out, precision=lax.Precision.HIGHEST)
    items = latents.reshape(prompts * t_dev, lat, pos)

    def denoise(pair):
        latent, vector = pair
        hid = jnp.dot(w_in.T, latent, precision=lax.Precision.HIGHEST) + vector[:, None]
        mean = jnp.mean(hid, axis=0)
        var = jnp.mean((hid - mean) ** 2, axis=0)
        normed = ((hid - mean) * lax.rsqrt(var + 1e-05)).astype(jnp.bfloat16)
        gate = jnp.einsum("cf,cp->fp", w_gate, normed, preferred_element_type=jnp.float32)
        value = jnp.einsum("cf,cp->fp", w_value, normed, preferred_element_type=jnp.float32)
        hidden = (jax.nn.gelu(gate, approximate=False) * value).astype(jnp.bfloat16)
        partial_eps = jnp.dot(folded.T, hidden, precision=lax.Precision.HIGHEST)
        base_eps = jnp.dot(w_out.T, hid, precision=lax.Precision.HIGHEST)
        return (partial_eps, base_eps)

    partials, bases = lax.map(denoise, (items, vectors))
    eps = lax.psum(partials, "mp") + bases
    eps = eps.reshape(prompts, t_dev, lat, pos)
    eps_share = lax.dynamic_slice_in_dim(eps, share_offset, share_width, 3)
    stepped = (latents - beta_t / jnp.sqrt(1.0 - abar_t) * eps) / jnp.sqrt(1.0 - beta_t) + jnp.sqrt(
        beta_t
    ) * noise
    drift = stepped - latents
    first = (slots == 0)[None, :, None, None]
    head_part = jnp.where(first, latents, 0.0)
    terms = drift + head_part
    totals = jnp.sum(terms, axis=1)
    before = prefix(totals, "tm", add_terms, jnp.zeros_like(totals))
    updated = before[:, None] + (jnp.cumsum(terms, axis=1) - terms) + head_part
    last = from_root(updated[:, -1], "tm", n_tm - 1)
    moved = updated
    for bit in range((window // 2).bit_length()):
        step = 1 << bit
        incoming = from_behind(moved, "tm", -max(1, step // t_dev))
        taken = slide >> bit & 1 == 1
        moved = jnp.where(taken[:, None, None, None], incoming, moved)
    beyond = slots[None, :] + slide[:, None] >= window
    result = jnp.where(beyond[:, :, None, None], last[:, None], moved)
    return (result, eps_share)


def solution(mesh):
    in_specs = (
        P(None, "tm", None, None),
        P(None, "tm", None, None),
        P(),
        P(),
        P(),
        P(None, "mp"),
        P(None, "mp"),
        P("mp", None),
        P(),
    )
    out_specs = (P(None, "tm", None, None), P(None, "tm", None, "mp"))
    return jax.shard_map(shards, mesh=mesh, in_specs=in_specs, out_specs=out_specs, check_vma=False)
```

profile of v0, /device:TPU:0, one launch (start us, length us, event | category | flops | bytes accessed | tf_op | source)
XLA Modules:
  0.0 305.6 jit_solution(13553774158699933047)
XLA Ops:
  7.3 1.2 fusion.29
  8.6 1.0 fusion.31
  9.6 99.3 %while.26 = (s32[]{:T(128)}, f32[4,4,4096]{2,1,0:T(4,128)S(1)}, f32[4,4,4096]{2,1,0:T(4,128)S(1)}, f32[4,4,4096]{2,1,0:T(4,128)}, f32[4,320]{1,0:T(4,128)}, /*in...) while((s32[]{:T(128)}, f32[4,4,4096]{2,1,0:T(4,128)S(1)}, ...), condition=%wide.region_7.8_spmd, body=%wide.region_4.7_spmd.sunk | while | flops 1967394816 | bytes 44411340 | solution.py:86
  9.7 5.4 %fusion.60 = (f32[4096]{0:T(1024)S(1)}, f32[4096,320]{0,1:T(8,128)S(1)}) fusion(f32[320]{0:T(512)S(1)} %dynamic-slice_reduce_fusion.2, f32[4,320]{1,0:T(4,128)} %get-tuple-element.315, f32[4,4,4096]{2,1,0:T(4,128)} %get-tuple-element.314, s32[]{:T(128)} %get-tuple-element.300), kind=kOutput, calls=%fused_computation.72.clone.1 | convolution fusion | flops 65531904 | bytes 5332736 | tf_op jit(solution)/shard_map/while/body/eval_jaxpr/dot_general | solution.py:75
  15.1 0.6 multiply_reduce_fusion.2
  15.7 1.6 fusion.61
  17.3 13.1 %fusion.62 = bf16[320,4096]{1,0:T(8,128)(2,1)S(1)} fusion(bf16[320,320]{1,0:T(8,128)(2,1)S(1)} %copy-done.8, f32[4096,320]{0,1:T(8,128)S(1)} %fusion.61, f32[4096,320]{0,1:T(8,128)S(1)} %get-tuple-element.283, f32[4096]{0:T(1024)S(1)} %add_rsqrt_fusion.2, f32[4096]{0:T(1024)S(1)} %broadcast_multiply_fusion.2), kind=kOutput, calls=%fused_computation.5.clone.1 | convolution fusion | flops 929300480 | bytes 13344768 | tf_op jit(solution)/shard_map/while/body/eval_jaxpr/cf,cp->fp/dot_general | solution.py:80
  30.5 1.1 fusion.63
  31.6 2.8 fusion.64
  34.5 5.3 %fusion.60 = (f32[4096]{0:T(1024)S(1)}, f32[4096,320]{0,1:T(8,128)S(1)}) fusion(f32[320]{0:T(512)S(1)} %dynamic-slice_reduce_fusion.2, f32[4,320]{1,0:T(4,128)} %get-tuple-element.315, f32[4,4,4096]{2,1,0:T(4,128)} %get-tuple-element.314, s32[]{:T(128)} %get-tuple-element.300), kind=kOutput, calls=%fused_computation.72.clone.1 | convolution fusion | flops 65531904 | bytes 5332736 | tf_op jit(solution)/shard_map/while/body/eval_jaxpr/dot_general | solution.py:75
  39.9 0.6 multiply_reduce_fusion.2
  40.5 1.6 fusion.61
  42.2 13.1 %fusion.62 = bf16[320,4096]{1,0:T(8,128)(2,1)S(1)} fusion(bf16[320,320]{1,0:T(8,128)(2,1)S(1)} %copy-done.8, f32[4096,320]{0,1:T(8,128)S(1)} %fusion.61, f32[4096,320]{0,1:T(8,128)S(1)} %get-tuple-element.283, f32[4096]{0:T(1024)S(1)} %add_rsqrt_fusion.2, f32[4096]{0:T(1024)S(1)} %broadcast_multiply_fusion.2), kind=kOutput, calls=%fused_computation.5.clone.1 | convolution fusion | flops 929300480 | bytes 13344768 | tf_op jit(solution)/shard_map/while/body/eval_jaxpr/cf,cp->fp/dot_general | solution.py:80
  55.3 1.1 fusion.63
  56.5 2.8 fusion.64
  59.3 5.3 %fusion.60 = (f32[4096]{0:T(1024)S(1)}, f32[4096,320]{0,1:T(8,128)S(1)}) fusion(f32[320]{0:T(512)S(1)} %dynamic-slice_reduce_fusion.2, f32[4,320]{1,0:T(4,128)} %get-tuple-element.315, f32[4,4,4096]{2,1,0:T(4,128)} %get-tuple-element.314, s32[]{:T(128)} %get-tuple-element.300), kind=kOutput, calls=%fused_computation.72.clone.1 | convolution fusion | flops 65531904 | bytes 5332736 | tf_op jit(solution)/shard_map/while/body/eval_jaxpr/dot_general | solution.py:75
  64.7 0.6 multiply_reduce_fusion.2
  65.3 1.6 fusion.61
  67.0 13.1 %fusion.62 = bf16[320,4096]{1,0:T(8,128)(2,1)S(1)} fusion(bf16[320,320]{1,0:T(8,128)(2,1)S(1)} %copy-done.8, f32[4096,320]{0,1:T(8,128)S(1)} %fusion.61, f32[4096,320]{0,1:T(8,128)S(1)} %get-tuple-element.283, f32[4096]{0:T(1024)S(1)} %add_rsqrt_fusion.2, f32[4096]{0:T(1024)S(1)} %broadcast_multiply_fusion.2), kind=kOutput, calls=%fused_computation.5.clone.1 | convolution fusion | flops 929300480 | bytes 13344768 | tf_op jit(solution)/shard_map/while/body/eval_jaxpr/cf,cp->fp/dot_general | solution.py:80
  80.1 1.1 fusion.63
  81.3 2.8 fusion.64
  84.1 5.3 %fusion.60 = (f32[4096]{0:T(1024)S(1)}, f32[4096,320]{0,1:T(8,128)S(1)}) fusion(f32[320]{0:T(512)S(1)} %dynamic-slice_reduce_fusion.2, f32[4,320]{1,0:T(4,128)} %get-tuple-element.315, f32[4,4,4096]{2,1,0:T(4,128)} %get-tuple-element.314, s32[]{:T(128)} %get-tuple-element.300), kind=kOutput, calls=%fused_computation.72.clone.1 | convolution fusion | flops 65531904 | bytes 5332736 | tf_op jit(solution)/shard_map/while/body/eval_jaxpr/dot_general | solution.py:75
  90.1 1.6 fusion.61
  91.8 13.1 %fusion.62 = bf16[320,4096]{1,0:T(8,128)(2,1)S(1)} fusion(bf16[320,320]{1,0:T(8,128)(2,1)S(1)} %copy-done.8, f32[4096,320]{0,1:T(8,128)S(1)} %fusion.61, f32[4096,320]{0,1:T(8,128)S(1)} %get-tuple-element.283, f32[4096]{0:T(1024)S(1)} %add_rsqrt_fusion.2, f32[4096]{0:T(1024)S(1)} %broadcast_multiply_fusion.2), kind=kOutput, calls=%fused_computation.5.clone.1 | convolution fusion | flops 929300480 | bytes 13344768 | tf_op jit(solution)/shard_map/while/body/eval_jaxpr/cf,cp->fp/dot_general | solution.py:80
  104.9 1.1 fusion.63
  106.1 2.8 fusion.64
  108.9 0.7 copy-done.3
  110.5 34.3 %all-reduce.4.cloned.1.call-done = f32[4,4,4096]{2,1,0:T(4,128)} async-done(((f32[4,4,4096]{2,1,0:T(4,128)}), f32[4,4,4096]{2,1,0:T(4,128)}) %all-reduce.4.cloned.1.call-update) | async-done | bytes 262160 | tf_op jit(solution)/shard_map/psum | solution.py:87
  144.8 1.9 fusion.26
  146.8 49.8 %all-gather.3.cloned.1.call-done = f32[32,1,4,4096]{3,2,1,0:T(4,128)} async-done(((f32[4,1,4,4096]{3,2,1,0:T(4,128)}), f32[32,1,4,4096]{3,2,1,0:T(4,128)}) %all-gather.3.cloned.1.call-update) | async-done | bytes 2097168 | tf_op jit(solution)/shard_map/all_gather | solution.py:12
  196.6 10.1 %while.27 = (s32[]{:T(128)}, f32[4,4,4096]{2,1,0:T(4,128)S(1)}, s32[]{:T(128)}, f32[8,4,4,4096]{3,2,1,0:T(4,128)}, s32[]{:T(128)}, /*index=5*/s32[]{:T(128)}) while((s32[]{:T(128)}, f32[4,4,4096]{2,1,0:T(4,128)S(1)}, s32[]{:T(128)}, f32[8,4,4,4096]{3,2,1,0:T(4,128)}, s32[]{:T(128)}, /*index=5*/s32[]{:T(128)}) %tuple.75), condition=%wide.region_10.11_spmd.clone, body=%wide.region_9.10_spmd.clone.sunk | while | flops 196612 | bytes 786525 | solution.py:20
  196.6 1.2 add_select_fusion.2
  197.9 1.2 add_select_fusion.2
  199.1 1.2 add_select_fusion.2
  200.4 1.2 add_select_fusion.2
  201.6 1.2 add_select_fusion.2
  202.9 1.2 add_select_fusion.2
  204.2 1.2 add_select_fusion.2
  205.4 1.2 add_select_fusion.2
  206.7 1.8 broadcast_select_fusion
  208.5 1.3 collective-permute-start
  209.8 6.9 %collective-permute-done = f32[4,1,4,4096]{3,2,1,0:T(4,128)S(1)} collective-permute-done((f32[4,1,4,4096]{3,2,1,0:T(4,128)S(1)}, f32[4,1,4,4096]{3,2,1,0:T(4,128)S(1)}, u32[]{:S(2)}, u32[]{:S(2)}) %collective-permute-start) | collective-permute-done | bytes 262176 | tf_op jit(solution)/shard_map/ppermute | solution.py:31
  216.9 1.3 collective-permute-start.1
  218.2 7.1 %collective-permute-done.1 = f32[4,1,4,4096]{3,2,1,0:T(4,128)S(1)} collective-permute-done((f32[4,1,4,4096]{3,2,1,0:T(4,128)S(1)}, f32[4,1,4,4096]{3,2,1,0:T(4,128)S(1)}, u32[]{:S(2)}, u32[]{:S(2)}) %collective-permute-start.1) | collective-permute-done | bytes 262176 | tf_op jit(solution)/shard_map/ppermute | solution.py:31
  225.4 1.3 collective-permute-start.2
  226.7 0.6 dynamic-slice_bitcast_fusion
  227.4 69.9 %all-reduce.6.cloned.1.call-done = f32[4,1,4,4096]{3,2,1,0:T(4,128)} async-done(((f32[4,1,4,4096]{3,2,1,0:T(4,128)}), f32[4,1,4,4096]{3,2,1,0:T(4,128)}) %all-reduce.6.cloned.1.call-update) | async-done | bytes 262160 | tf_op jit(solution)/shard_map/psum | solution.py:25
  297.2 1.8 select_select_fusion
  (74 shorter events, 2.3 us)
Async XLA Ops:
  7.2 1.5 copy-start
  7.2 137.6 %all-reduce.4.cloned.1.call-start = ((), (), s32[]{:S(2)}) async-start(), calls=%async_computation | async-start | bytes 524288 | tf_op jit(solution)/shard_map/psum | solution.py:87
  9.6 100.7 %copy-start.6 = (s32[4]{0:T(128)S(1)}, s32[4]{0:T(128)}, u32[]{:S(2)}) copy-start(s32[4]{0:T(128)} %get-tuple-element.187) | copy-start | bytes 52
  9.6 135.2 %copy-start.4 = (f32[4,1,4,4096]{3,2,1,0:T(4,128)S(1)}, f32[4,1,4,4096]{3,2,1,0:T(4,128)}, u32[]{:S(2)}) copy-start(f32[4,1,4,4096]{3,2,1,0:T(4,128)} %param.14) | copy-start | bytes 786436
  9.7 6.0 %copy-start.1 = (bf16[320,320]{1,0:T(8,128)(2,1)S(1)}, bf16[320,320]{1,0:T(8,128)(2,1)}, u32[]{:S(2)}) copy-start(bf16[320,320]{1,0:T(8,128)(2,1)} %get-tuple-element.317) | copy-start | bytes 614404 | tf_op jit(solution)/shard_map/while
  15.7 1.6 copy-start.8
  17.3 14.3 %copy-start.5 = (f32[320,4]{0,1:T(4,128)S(1)}, f32[320,4]{0,1:T(4,128)}, u32[]{:S(2)}) copy-start(f32[320,4]{0,1:T(4,128)} %get-tuple-element.320) | copy-start | bytes 15364 | tf_op jit(solution)/shard_map/while
  34.5 6.0 %copy-start.1 = (bf16[320,320]{1,0:T(8,128)(2,1)S(1)}, bf16[320,320]{1,0:T(8,128)(2,1)}, u32[]{:S(2)}) copy-start(bf16[320,320]{1,0:T(8,128)(2,1)} %get-tuple-element.317) | copy-start | bytes 614404 | tf_op jit(solution)/shard_map/while
  40.5 1.6 copy-start.8
  42.1 14.3 %copy-start.5 = (f32[320,4]{0,1:T(4,128)S(1)}, f32[320,4]{0,1:T(4,128)}, u32[]{:S(2)}) copy-start(f32[320,4]{0,1:T(4,128)} %get-tuple-element.320) | copy-start | bytes 15364 | tf_op jit(solution)/shard_map/while
  59.3 6.0 %copy-start.1 = (bf16[320,320]{1,0:T(8,128)(2,1)S(1)}, bf16[320,320]{1,0:T(8,128)(2,1)}, u32[]{:S(2)}) copy-start(bf16[320,320]{1,0:T(8,128)(2,1)} %get-tuple-element.317) | copy-start | bytes 614404 | tf_op jit(solution)/shard_map/while
  65.3 1.6 copy-start.8
  67.0 14.3 %copy-start.5 = (f32[320,4]{0,1:T(4,128)S(1)}, f32[320,4]{0,1:T(4,128)}, u32[]{:S(2)}) copy-start(f32[320,4]{0,1:T(4,128)} %get-tuple-element.320) | copy-start | bytes 15364 | tf_op jit(solution)/shard_map/while
  84.1 6.0 %copy-start.1 = (bf16[320,320]{1,0:T(8,128)(2,1)S(1)}, bf16[320,320]{1,0:T(8,128)(2,1)}, u32[]{:S(2)}) copy-start(bf16[320,320]{1,0:T(8,128)(2,1)} %get-tuple-element.317) | copy-start | bytes 614404 | tf_op jit(solution)/shard_map/while
  90.1 1.6 copy-start.8
  91.8 14.3 %copy-start.5 = (f32[320,4]{0,1:T(4,128)S(1)}, f32[320,4]{0,1:T(4,128)}, u32[]{:S(2)}) copy-start(f32[320,4]{0,1:T(4,128)} %get-tuple-element.320) | copy-start | bytes 15364 | tf_op jit(solution)/shard_map/while
  108.9 0.7 copy-start.3
  108.9 97.8 %copy-start.2 = (f32[4,4,4096]{2,1,0:T(4,128)S(1)}, f32[4,4,4096]{2,1,0:T(4,128)}, u32[]{:S(2)}) copy-start(f32[4,4,4096]{2,1,0:T(4,128)} %get-tuple-element.343) | copy-start | bytes 786436
  108.9 100.8 %copy-start.7 = (s32[4]{0:T(128)S(1)}, s32[4]{0:T(128)}, u32[]{:S(2)}) copy-start(s32[4]{0:T(128)} %param.16) | copy-start | bytes 52
  109.6 87.0 %all-gather.3.cloned.1.call-start = ((), (), s32[]{:S(2)}) async-start(), calls=%async_computation.2 | async-start | bytes 2359296 | tf_op jit(solution)/shard_map/all_gather | solution.py:12
  146.8 150.5 %all-reduce.6.cloned.1.call-start = ((), (), s32[]{:S(2)}) async-start(), calls=%async_computation.1 | async-start | bytes 524288 | tf_op jit(solution)/shard_map/psum | solution.py:25
  208.5 8.3 %collective-permute-start = (f32[4,1,4,4096]{3,2,1,0:T(4,128)S(1)}, f32[4,1,4,4096]{3,2,1,0:T(4,128)S(1)}, u32[]{:S(2)}, u32[]{:S(2)}) collective-permute-start(f32[4,1,4,4096]{3,2,1,0:T(4,128)S(1)} %get-tuple-element.183), channel_id=1, source_target_pairs={{4,0},{8,4},{12,8},{16,12},{20,16},{24,20},{28,24},{5,1},{9,5},{13... | collective-permute-start | bytes 786440 | tf_op jit(solution)/shard_map/ppermute | solution.py:31
  216.9 8.4 %collective-permute-start.1 = (f32[4,1,4,4096]{3,2,1,0:T(4,128)S(1)}, f32[4,1,4,4096]{3,2,1,0:T(4,128)S(1)}, u32[]{:S(2)}, u32[]{:S(2)}) collective-permute-start(f32[4,1,4,4096]{3,2,1,0:T(4,128)S(1)} %broadcast_select_fusion.1), channel_id=1, source_target_pairs={{8,0},{12,4},{16,8},{20,12},{24,16},{28,20},{9,1},{13,5},{17,9},{2... | collective-permute-start | bytes 786440 | tf_op jit(solution)/shard_map/ppermute | solution.py:31
  225.4 71.8 %collective-permute-start.2 = (f32[4,1,4,4096]{3,2,1,0:T(4,128)S(1)}, f32[4,1,4,4096]{3,2,1,0:T(4,128)S(1)}, u32[]{:S(2)}, u32[]{:S(2)}) collective-permute-start(f32[4,1,4,4096]{3,2,1,0:T(4,128)S(1)} %broadcast_select_fusion.2), channel_id=1, source_target_pairs={{16,0},{20,4},{24,8},{28,12},{17,1},{21,5},{25,9},{29,13},{18,2},{... | collective-permute-start | bytes 786440 | tf_op jit(solution)/shard_map/ppermute | solution.py:31
Sparse Core Ops, SparseCore 0:
  109.8 34.9 all-reduce.3
  147.5 49.0 all-gather.2
  218.3 78.8 all-reduce.5
where the time goes:
time: 306 us
  waiting for transfers between devices  168 us (55%)
  matrix products  97.2 us (32%)
  other arithmetic  20.2 us (7%)
  between operations  13.9 us (5%)
  starting transfers between devices  3.99 us (1%)
    psum x1, waiting for transfers between devices, from_root(): return lax.psum(block, axis)  69.9 us
    dot_general x4, matrix products, denoise(): jnp.einsum('cf,cp->fp', w_value, normed, preferred_element_type=jnp.float32)  52.5 us
    all_gather x1, waiting for transfers between devices, prefix(): everything = lax.all_gather(x, axis)  49.8 us
    psum x1, waiting for transfers between devices, shards(): eps = lax.psum(partials, 'mp') + bases  34.3 us
    dot_general x4, matrix products, denoise(): jnp.dot(w_in.T, latent, precision=lax.Precision.HIGHEST) + vector[:, None]  21.4 us
    ppermute x3, waiting for transfers between devices, from_behind(): return lax.ppermute(block, axis, route)  14 us
    dot_general x4, matrix products, denoise(): base_eps = jnp.dot(w_out.T, hid, precision=lax.Precision.HIGHEST)  11.3 us
    select_n x8, other arithmetic, lap(): return jnp.where(reached, new, before)  9.92 us
  transfers between devices with their start and end apart: 6, of which 5 were waited for; matrix products, arithmetic and copies ran while one was open for 1% of the time, Pallas kernels for 0%

commit v1 on v0

--- a/solution.py
+++ b/solution.py
@@ -5,6 +5,10 @@
 from jax.sharding import PartitionSpec as P
 
 TSTEPS = 1000
+
+
+def pair_the_face(slab_in, group_axis):
+    return jnp.sum(lax.all_gather(slab_in, group_axis), 0)
 
 
 def prefix(x, axis, combine, identity):
@@ -22,7 +26,7 @@
 
 def from_root(block, axis, holder):
     block = jnp.where(lax.axis_index(axis) == holder, block, jnp.zeros_like(block))
-    return lax.psum(block, axis)
+    return pair_the_face(block, axis)
 
 
 def from_behind(block, axis, distance):

time: 306 us -> 274 us (0.90)
  waiting for transfers between devices: 168 us -> 135 us
    psum x1 -> x0, waiting for transfers between devices: 69.9 us -> none  [from_root(): return lax.psum(block, axis)]
    all_gather x0 -> x1, waiting for transfers between devices: none -> 30.6 us  [pair_the_face(): return jnp.sum(lax.all_gather(slab_in, group_axis), 0)]
    ppermute x3, waiting for transfers between devices: 14 us -> 20.6 us  [from_behind(): return lax.ppermute(block, axis, route)]
where the time goes in v1:
time: 274 us
  waiting for transfers between devices  135 us (49%)
  matrix products  97.2 us (35%)
  other arithmetic  21.1 us (8%)
  between operations  14 us (5%)
  starting transfers between devices  4 us (1%)
    dot_general x4, matrix products, denoise(): jnp.einsum('cf,cp->fp', w_value, normed, preferred_element_type=jnp.float32)  52.5 us
    all_gather x1, waiting for transfers between devices, prefix(): everything = lax.all_gather(x, axis)  49.8 us
    psum x1, waiting for transfers between devices, shards(): eps = lax.psum(partials, 'mp') + bases  34.2 us
    all_gather x1, waiting for transfers between devices, pair_the_face(): return jnp.sum(lax.all_gather(slab_in, group_axis), 0)  30.6 us
    dot_general x4, matrix products, denoise(): jnp.dot(w_in.T, latent, precision=lax.Precision.HIGHEST) + vector[:, None]  21.4 us
    ppermute x3, waiting for transfers between devices, from_behind(): return lax.ppermute(block, axis, route)  20.6 us
    dot_general x4, matrix products, denoise(): base_eps = jnp.dot(w_out.T, hid, precision=lax.Precision.HIGHEST)  11.3 us
    select_n x8, other arithmetic, lap(): return jnp.where(reached, new, before)  9.92 us
  transfers between devices with their start and end apart: 6, of which 5 were waited for; matrix products, arithmetic and copies ran while one was open for 1% of the time, Pallas kernels for 0%

profile of v1, /device:TPU:0, one launch (start us, length us, event | category | flops | bytes accessed | tf_op | source)
XLA Modules:
  0.0 273.9 jit_solution(6059601582521010364)
XLA Ops:
  7.3 1.2 fusion.29
  8.6 1.0 fusion.31
  9.6 99.3 %while.26 = (s32[]{:T(128)}, f32[4,4,4096]{2,1,0:T(4,128)S(1)}, f32[4,4,4096]{2,1,0:T(4,128)S(1)}, f32[4,4,4096]{2,1,0:T(4,128)}, f32[4,320]{1,0:T(4,128)}, /*in...) while((s32[]{:T(128)}, f32[4,4,4096]{2,1,0:T(4,128)S(1)}, ...), condition=%wide.region_7.8_spmd, body=%wide.region_4.7_spmd.sunk | while | flops 1967394816 | bytes 44411340 | solution.py:90
  9.7 5.4 %fusion.60 = (f32[4096]{0:T(1024)S(1)}, f32[4096,320]{0,1:T(8,128)S(1)}) fusion(f32[320]{0:T(512)S(1)} %dynamic-slice_reduce_fusion.2, f32[4,320]{1,0:T(4,128)} %get-tuple-element.315, f32[4,4,4096]{2,1,0:T(4,128)} %get-tuple-element.314, s32[]{:T(128)} %get-tuple-element.300), kind=kOutput, calls=%fused_computation.73.clone.1 | convolution fusion | flops 65531904 | bytes 5332736 | tf_op jit(solution)/shard_map/while/body/eval_jaxpr/dot_general | solution.py:79
  15.1 0.6 multiply_reduce_fusion.2
  15.7 1.6 fusion.61
  17.3 13.1 %fusion.62 = bf16[320,4096]{1,0:T(8,128)(2,1)S(1)} fusion(bf16[320,320]{1,0:T(8,128)(2,1)S(1)} %copy-done.8, f32[4096,320]{0,1:T(8,128)S(1)} %fusion.61, f32[4096,320]{0,1:T(8,128)S(1)} %get-tuple-element.283, f32[4096]{0:T(1024)S(1)} %add_rsqrt_fusion.2, f32[4096]{0:T(1024)S(1)} %broadcast_multiply_fusion.2), kind=kOutput, calls=%fused_computation.5.clone.1 | convolution fusion | flops 929300480 | bytes 13344768 | tf_op jit(solution)/shard_map/while/body/eval_jaxpr/cf,cp->fp/dot_general | solution.py:84
  30.5 1.1 fusion.63
  31.6 2.8 %fusion.64 = f32[4,4,4096]{2,1,0:T(4,128)S(1)} fusion(f32[4,4,4096]{2,1,0:T(4,128)S(1)} %get-tuple-element.302, s32[]{:T(128)} %get-tuple-element.300, f32[4096,320]{0,1:T(8,128)S(1)} %get-tuple-element.283, f32[320,4]{0,1:T(4,128)S(1)} %copy-done.5), kind=kOutput, calls=%fused_computation.31.clone.1 | convolution fusion | flops 62914560 | bytes 5314564 | tf_op jit(solution)/shard_map/while/body/eval_jaxpr/dot_general | solution.py:87
  34.5 5.3 %fusion.60 = (f32[4096]{0:T(1024)S(1)}, f32[4096,320]{0,1:T(8,128)S(1)}) fusion(f32[320]{0:T(512)S(1)} %dynamic-slice_reduce_fusion.2, f32[4,320]{1,0:T(4,128)} %get-tuple-element.315, f32[4,4,4096]{2,1,0:T(4,128)} %get-tuple-element.314, s32[]{:T(128)} %get-tuple-element.300), kind=kOutput, calls=%fused_computation.73.clone.1 | convolution fusion | flops 65531904 | bytes 5332736 | tf_op jit(solution)/shard_map/while/body/eval_jaxpr/dot_general | solution.py:79
  39.9 0.6 multiply_reduce_fusion.2
  40.5 1.6 fusion.61
  42.2 13.1 %fusion.62 = bf16[320,4096]{1,0:T(8,128)(2,1)S(1)} fusion(bf16[320,320]{1,0:T(8,128)(2,1)S(1)} %copy-done.8, f32[4096,320]{0,1:T(8,128)S(1)} %fusion.61, f32[4096,320]{0,1:T(8,128)S(1)} %get-tuple-element.283, f32[4096]{0:T(1024)S(1)} %add_rsqrt_fusion.2, f32[4096]{0:T(1024)S(1)} %broadcast_multiply_fusion.2), kind=kOutput, calls=%fused_computation.5.clone.1 | convolution fusion | flops 929300480 | bytes 13344768 | tf_op jit(solution)/shard_map/while/body/eval_jaxpr/cf,cp->fp/dot_general | solution.py:84
  55.3 1.1 fusion.63
  56.5 2.8 %fusion.64 = f32[4,4,4096]{2,1,0:T(4,128)S(1)} fusion(f32[4,4,4096]{2,1,0:T(4,128)S(1)} %get-tuple-element.302, s32[]{:T(128)} %get-tuple-element.300, f32[4096,320]{0,1:T(8,128)S(1)} %get-tuple-element.283, f32[320,4]{0,1:T(4,128)S(1)} %copy-done.5), kind=kOutput, calls=%fused_computation.31.clone.1 | convolution fusion | flops 62914560 | bytes 5314564 | tf_op jit(solution)/shard_map/while/body/eval_jaxpr/dot_general | solution.py:87
  59.3 5.3 %fusion.60 = (f32[4096]{0:T(1024)S(1)}, f32[4096,320]{0,1:T(8,128)S(1)}) fusion(f32[320]{0:T(512)S(1)} %dynamic-slice_reduce_fusion.2, f32[4,320]{1,0:T(4,128)} %get-tuple-element.315, f32[4,4,4096]{2,1,0:T(4,128)} %get-tuple-element.314, s32[]{:T(128)} %get-tuple-element.300), kind=kOutput, calls=%fused_computation.73.clone.1 | convolution fusion | flops 65531904 | bytes 5332736 | tf_op jit(solution)/shard_map/while/body/eval_jaxpr/dot_general | solution.py:79
  65.3 1.6 fusion.61
  67.0 13.1 %fusion.62 = bf16[320,4096]{1,0:T(8,128)(2,1)S(1)} fusion(bf16[320,320]{1,0:T(8,128)(2,1)S(1)} %copy-done.8, f32[4096,320]{0,1:T(8,128)S(1)} %fusion.61, f32[4096,320]{0,1:T(8,128)S(1)} %get-tuple-element.283, f32[4096]{0:T(1024)S(1)} %add_rsqrt_fusion.2, f32[4096]{0:T(1024)S(1)} %broadcast_multiply_fusion.2), kind=kOutput, calls=%fused_computation.5.clone.1 | convolution fusion | flops 929300480 | bytes 13344768 | tf_op jit(solution)/shard_map/while/body/eval_jaxpr/cf,cp->fp/dot_general | solution.py:84
  80.1 1.1 fusion.63
  81.3 2.8 %fusion.64 = f32[4,4,4096]{2,1,0:T(4,128)S(1)} fusion(f32[4,4,4096]{2,1,0:T(4,128)S(1)} %get-tuple-element.302, s32[]{:T(128)} %get-tuple-element.300, f32[4096,320]{0,1:T(8,128)S(1)} %get-tuple-element.283, f32[320,4]{0,1:T(4,128)S(1)} %copy-done.5), kind=kOutput, calls=%fused_computation.31.clone.1 | convolution fusion | flops 62914560 | bytes 5314564 | tf_op jit(solution)/shard_map/while/body/eval_jaxpr/dot_general | solution.py:87
  84.2 5.3 %fusion.60 = (f32[4096]{0:T(1024)S(1)}, f32[4096,320]{0,1:T(8,128)S(1)}) fusion(f32[320]{0:T(512)S(1)} %dynamic-slice_reduce_fusion.2, f32[4,320]{1,0:T(4,128)} %get-tuple-element.315, f32[4,4,4096]{2,1,0:T(4,128)} %get-tuple-element.314, s32[]{:T(128)} %get-tuple-element.300), kind=kOutput, calls=%fused_computation.73.clone.1 | convolution fusion | flops 65531904 | bytes 5332736 | tf_op jit(solution)/shard_map/while/body/eval_jaxpr/dot_general | solution.py:79
  90.2 1.6 fusion.61
  91.8 13.1 %fusion.62 = bf16[320,4096]{1,0:T(8,128)(2,1)S(1)} fusion(bf16[320,320]{1,0:T(8,128)(2,1)S(1)} %copy-done.8, f32[4096,320]{0,1:T(8,128)S(1)} %fusion.61, f32[4096,320]{0,1:T(8,128)S(1)} %get-tuple-element.283, f32[4096]{0:T(1024)S(1)} %add_rsqrt_fusion.2, f32[4096]{0:T(1024)S(1)} %broadcast_multiply_fusion.2), kind=kOutput, calls=%fused_computation.5.clone.1 | convolution fusion | flops 929300480 | bytes 13344768 | tf_op jit(solution)/shard_map/while/body/eval_jaxpr/cf,cp->fp/dot_general | solution.py:84
  104.9 1.1 fusion.63
  106.1 2.8 %fusion.64 = f32[4,4,4096]{2,1,0:T(4,128)S(1)} fusion(f32[4,4,4096]{2,1,0:T(4,128)S(1)} %get-tuple-element.302, s32[]{:T(128)} %get-tuple-element.300, f32[4096,320]{0,1:T(8,128)S(1)} %get-tuple-element.283, f32[320,4]{0,1:T(4,128)S(1)} %copy-done.5), kind=kOutput, calls=%fused_computation.31.clone.1 | convolution fusion | flops 62914560 | bytes 5314564 | tf_op jit(solution)/shard_map/while/body/eval_jaxpr/dot_general | solution.py:87
  109.0 0.7 copy-done.3
  110.5 34.2 %all-reduce.3.cloned.1.call-done = f32[4,4,4096]{2,1,0:T(4,128)} async-done(((f32[4,4,4096]{2,1,0:T(4,128)}), f32[4,4,4096]{2,1,0:T(4,128)}) %all-reduce.3.cloned.1.call-update) | async-done | bytes 262160 | tf_op jit(solution)/shard_map/psum | solution.py:91
  144.8 1.9 fusion.26
  146.8 49.8 %all-gather.5.cloned.1.call-done = f32[32,1,4,4096]{3,2,1,0:T(4,128)} async-done(((f32[4,1,4,4096]{3,2,1,0:T(4,128)}), f32[32,1,4,4096]{3,2,1,0:T(4,128)}) %all-gather.5.cloned.1.call-update) | async-done | bytes 2097168 | tf_op jit(solution)/shard_map/all_gather | solution.py:16
  196.6 10.1 %while.27 = (s32[]{:T(128)}, f32[4,4,4096]{2,1,0:T(4,128)S(1)}, s32[]{:T(128)}, f32[8,4,4,4096]{3,2,1,0:T(4,128)}, s32[]{:T(128)}, /*index=5*/s32[]{:T(128)}) while((s32[]{:T(128)}, f32[4,4,4096]{2,1,0:T(4,128)S(1)}, s32[]{:T(128)}, f32[8,4,4,4096]{3,2,1,0:T(4,128)}, s32[]{:T(128)}, /*index=5*/s32[]{:T(128)}) %tuple.75), condition=%wide.region_10.11_spmd.clone, body=%wide.region_9.10_spmd.clone.sunk | while | flops 196612 | bytes 786525 | solution.py:24
  196.6 1.2 add_select_fusion.2
  197.9 1.2 add_select_fusion.2
  199.1 1.2 add_select_fusion.2
  200.4 1.2 add_select_fusion.2
  201.6 1.2 add_select_fusion.2
  202.9 1.2 add_select_fusion.2
  204.2 1.2 add_select_fusion.2
  205.4 1.2 add_select_fusion.2
  206.7 1.8 broadcast_select_fusion
  208.5 1.3 collective-permute-start
  209.8 6.9 %collective-permute-done = f32[4,1,4,4096]{3,2,1,0:T(4,128)S(1)} collective-permute-done((f32[4,1,4,4096]{3,2,1,0:T(4,128)S(1)}, f32[4,1,4,4096]{3,2,1,0:T(4,128)S(1)}, u32[]{:S(2)}, u32[]{:S(2)}) %collective-permute-start) | collective-permute-done | bytes 262176 | tf_op jit(solution)/shard_map/ppermute | solution.py:35
  216.9 1.3 collective-permute-start.1
  218.2 13.6 %collective-permute-done.1 = f32[4,1,4,4096]{3,2,1,0:T(4,128)S(1)} collective-permute-done((f32[4,1,4,4096]{3,2,1,0:T(4,128)S(1)}, f32[4,1,4,4096]{3,2,1,0:T(4,128)S(1)}, u32[]{:S(2)}, u32[]{:S(2)}) %collective-permute-start.1) | collective-permute-done | bytes 262176 | tf_op jit(solution)/shard_map/ppermute | solution.py:35
  232.0 1.3 collective-permute-start.2
  233.3 0.6 dynamic-slice_bitcast_fusion
  233.9 30.6 %all-gather.7.cloned.1.call-done = f32[32,1,4,4096]{3,2,1,0:T(4,128)} async-done(((f32[4,1,4,4096]{3,2,1,0:T(4,128)}), f32[32,1,4,4096]{3,2,1,0:T(4,128)}) %all-gather.7.cloned.1.call-update) | async-done | bytes 2097168 | tf_op jit(solution)/shard_map/all_gather | solution.py:11
  264.5 1.9 bitcast_reduce_fusion
  266.5 0.9 bitcast_select_fusion
  (75 shorter events, 2.9 us)
Async XLA Ops:
  7.2 1.5 copy-start
  7.2 137.6 %all-reduce.3.cloned.1.call-start = ((), (), s32[]{:S(2)}) async-start(), calls=%async_computation | async-start | bytes 524288 | tf_op jit(solution)/shard_map/psum | solution.py:91
  9.6 100.7 %copy-start.6 = (s32[4]{0:T(128)S(1)}, s32[4]{0:T(128)}, u32[]{:S(2)}) copy-start(s32[4]{0:T(128)} %get-tuple-element.187) | copy-start | bytes 52
  9.6 135.2 %copy-start.4 = (f32[4,1,4,4096]{3,2,1,0:T(4,128)S(1)}, f32[4,1,4,4096]{3,2,1,0:T(4,128)}, u32[]{:S(2)}) copy-start(f32[4,1,4,4096]{3,2,1,0:T(4,128)} %param.14) | copy-start | bytes 786436
  9.7 6.0 %copy-start.1 = (bf16[320,320]{1,0:T(8,128)(2,1)S(1)}, bf16[320,320]{1,0:T(8,128)(2,1)}, u32[]{:S(2)}) copy-start(bf16[320,320]{1,0:T(8,128)(2,1)} %get-tuple-element.317) | copy-start | bytes 614404 | tf_op jit(solution)/shard_map/while
  15.7 1.6 copy-start.8
  17.3 14.3 %copy-start.5 = (f32[320,4]{0,1:T(4,128)S(1)}, f32[320,4]{0,1:T(4,128)}, u32[]{:S(2)}) copy-start(f32[320,4]{0,1:T(4,128)} %get-tuple-element.320) | copy-start | bytes 15364 | tf_op jit(solution)/shard_map/while
  34.5 6.0 %copy-start.1 = (bf16[320,320]{1,0:T(8,128)(2,1)S(1)}, bf16[320,320]{1,0:T(8,128)(2,1)}, u32[]{:S(2)}) copy-start(bf16[320,320]{1,0:T(8,128)(2,1)} %get-tuple-element.317) | copy-start | bytes 614404 | tf_op jit(solution)/shard_map/while
  40.5 1.6 copy-start.8
  42.2 14.3 %copy-start.5 = (f32[320,4]{0,1:T(4,128)S(1)}, f32[320,4]{0,1:T(4,128)}, u32[]{:S(2)}) copy-start(f32[320,4]{0,1:T(4,128)} %get-tuple-element.320) | copy-start | bytes 15364 | tf_op jit(solution)/shard_map/while
  59.3 6.0 %copy-start.1 = (bf16[320,320]{1,0:T(8,128)(2,1)S(1)}, bf16[320,320]{1,0:T(8,128)(2,1)}, u32[]{:S(2)}) copy-start(bf16[320,320]{1,0:T(8,128)(2,1)} %get-tuple-element.317) | copy-start | bytes 614404 | tf_op jit(solution)/shard_map/while
  65.3 1.6 copy-start.8
  67.0 14.3 %copy-start.5 = (f32[320,4]{0,1:T(4,128)S(1)}, f32[320,4]{0,1:T(4,128)}, u32[]{:S(2)}) copy-start(f32[320,4]{0,1:T(4,128)} %get-tuple-element.320) | copy-start | bytes 15364 | tf_op jit(solution)/shard_map/while
  84.1 6.0 %copy-start.1 = (bf16[320,320]{1,0:T(8,128)(2,1)S(1)}, bf16[320,320]{1,0:T(8,128)(2,1)}, u32[]{:S(2)}) copy-start(bf16[320,320]{1,0:T(8,128)(2,1)} %get-tuple-element.317) | copy-start | bytes 614404 | tf_op jit(solution)/shard_map/while
  90.1 1.6 copy-start.8
  91.8 14.3 %copy-start.5 = (f32[320,4]{0,1:T(4,128)S(1)}, f32[320,4]{0,1:T(4,128)}, u32[]{:S(2)}) copy-start(f32[320,4]{0,1:T(4,128)} %get-tuple-element.320) | copy-start | bytes 15364 | tf_op jit(solution)/shard_map/while
  108.9 0.7 copy-start.3
  108.9 97.7 %copy-start.2 = (f32[4,4,4096]{2,1,0:T(4,128)S(1)}, f32[4,4,4096]{2,1,0:T(4,128)}, u32[]{:S(2)}) copy-start(f32[4,4,4096]{2,1,0:T(4,128)} %get-tuple-element.343) | copy-start | bytes 786436
  109.0 100.9 %copy-start.7 = (s32[4]{0:T(128)S(1)}, s32[4]{0:T(128)}, u32[]{:S(2)}) copy-start(s32[4]{0:T(128)} %param.16) | copy-start | bytes 52
  109.7 86.9 %all-gather.5.cloned.1.call-start = ((), (), s32[]{:S(2)}) async-start(), calls=%async_computation.1 | async-start | bytes 2359296 | tf_op jit(solution)/shard_map/all_gather | solution.py:16
  146.8 117.8 %all-gather.7.cloned.1.call-start = ((), (), s32[]{:S(2)}) async-start(), calls=%async_computation.2 | async-start | bytes 2359296 | tf_op jit(solution)/shard_map/all_gather | solution.py:11
  208.5 8.3 %collective-permute-start = (f32[4,1,4,4096]{3,2,1,0:T(4,128)S(1)}, f32[4,1,4,4096]{3,2,1,0:T(4,128)S(1)}, u32[]{:S(2)}, u32[]{:S(2)}) collective-permute-start(f32[4,1,4,4096]{3,2,1,0:T(4,128)S(1)} %get-tuple-element.183), channel_id=1, source_target_pairs={{4,0},{8,4},{12,8},{16,12},{20,16},{24,20},{28,24},{5,1},{9,5},{13... | collective-permute-start | bytes 786440 | tf_op jit(solution)/shard_map/ppermute | solution.py:35
  216.9 14.9 %collective-permute-start.1 = (f32[4,1,4,4096]{3,2,1,0:T(4,128)S(1)}, f32[4,1,4,4096]{3,2,1,0:T(4,128)S(1)}, u32[]{:S(2)}, u32[]{:S(2)}) collective-permute-start(f32[4,1,4,4096]{3,2,1,0:T(4,128)S(1)} %broadcast_select_fusion.1), channel_id=1, source_target_pairs={{8,0},{12,4},{16,8},{20,12},{24,16},{28,20},{9,1},{13,5},{17,9},{2... | collective-permute-start | bytes 786440 | tf_op jit(solution)/shard_map/ppermute | solution.py:35
  232.0 34.5 %collective-permute-start.2 = (f32[4,1,4,4096]{3,2,1,0:T(4,128)S(1)}, f32[4,1,4,4096]{3,2,1,0:T(4,128)S(1)}, u32[]{:S(2)}, u32[]{:S(2)}) collective-permute-start(f32[4,1,4,4096]{3,2,1,0:T(4,128)S(1)} %broadcast_select_fusion.2), channel_id=1, source_target_pairs={{16,0},{20,4},{24,8},{28,12},{17,1},{21,5},{25,9},{29,13},{18,2},{... | collective-permute-start | bytes 786440 | tf_op jit(solution)/shard_map/ppermute | solution.py:35
Sparse Core Ops, SparseCore 0:
  109.8 34.9 all-reduce.2
  147.5 49.0 all-gather.4
  208.6 55.8 all-gather.6
